TPU v7x, 32 devices: a 4x4x1 block of a 4x4x8 slice. The times are simulated.
32 devices in a mesh: rep: 1 (over z), data: 4 (over y), model: 8 (over x, core).
Axes of the slice: x: 4, y: 4, z: 1, core: 2. Of those that a mesh axis runs over, the one named last changes fastest.
The devices are a block of a 4x4x8 slice.
Arguments:
- x_in: bfloat16 [8, 1024, 4096], P(('rep', 'data'), 'model')
- key_lens: int32 [8], P(('rep', 'data'))
- ln_gain: bfloat16 [2, 4096], P(None, 'data')
- w_in: bfloat16 [2, 4096, 38912], P(None, 'data', 'model')
- w_out_attn: bfloat16 [2, 4096, 4096], P(None, 'model', 'data')
- w_out_mlp: bfloat16 [2, 16384, 4096], P(None, 'model', 'data')
Outputs:
- output: bfloat16 [8, 1024, 4096], P(('rep', 'data'), 'model')
All inputs are finite; a program needn't handle non-finite values.
Results may differ from a plain program's by a relative error of at most 0.0171249.
Values are sent between devices in bfloat16 or wider.
A program may use at most 768 MiB of HBM per device.

v0:
```python
import jax
import jax.numpy as jnp
from jax import lax
from jax.sharding import PartitionSpec as P, NamedSharding

EPSILON = 1e-6


def layer_norm(act_in, gain_vec):
    act_f32 = act_in.astype(jnp.float32)
    row_mean = jnp.mean(act_f32, axis=-1, keepdims=True)
    centered = act_f32 - row_mean
    row_var = jnp.mean(centered * centered, axis=-1, keepdims=True)
    return (centered * lax.rsqrt(row_var + EPSILON) * gain_vec.astype(jnp.float32)).astype(jnp.bfloat16)


def solution(mesh):
    n_groups = mesh.shape['model']
    batch_axes = ('rep', 'data')

    def device_step(x_loc, len_loc, gain_loc, w_in_loc, w_attn_loc, w_mlp_loc):
        n_layers = w_in_loc.shape[0]
        block_in = w_in_loc.shape[2]
        attn_width = w_attn_loc.shape[1]
        ff_local = w_mlp_loc.shape[1]
        head_dim = (block_in - attn_width - 2 * ff_local) // 2
        q_group = attn_width // head_dim
        batch_loc, seq_loc = x_loc.shape[0], x_loc.shape[1]
        seq_len = seq_loc * n_groups
        kv_start = attn_width
        ff_start = attn_width + 2 * head_dim
        positions = jnp.arange(seq_len)
        allowed = (positions[None, :] <= positions[:, None])[None, :, :] & (positions[None, None, :] < len_loc[:, None, None])
        allowed = allowed[:, None, :, :]
        hidden = x_loc
        for layer_idx in range(n_layers):
            gain_full = lax.all_gather(gain_loc[layer_idx], 'data', axis=0, tiled=True)
            w_in_full = lax.all_gather(w_in_loc[layer_idx], 'data', axis=0, tiled=True)
            w_attn_full = lax.all_gather(w_attn_loc[layer_idx], 'data', axis=1, tiled=True)
            w_mlp_full = lax.all_gather(w_mlp_loc[layer_idx], 'data', axis=1, tiled=True)
            normed = layer_norm(hidden, gain_full)
            h_full = lax.all_gather(normed, 'model', axis=1, tiled=True)
            projected = jnp.dot(h_full, w_in_full, preferred_element_type=jnp.float32).astype(jnp.bfloat16)
            queries = projected[:, :, :attn_width].reshape(batch_loc, seq_len, q_group, head_dim)
            key_head = projected[:, :, kv_start:kv_start + head_dim]
            value_head = projected[:, :, kv_start + head_dim:ff_start]
            gate_proj = projected[:, :, ff_start:ff_start + ff_local]
            up_proj = projected[:, :, ff_start + ff_local:]
            scores = jnp.einsum('crke,cle->ckrl', queries, key_head, preferred_element_type=jnp.float32) * head_dim ** -0.5
            scores = jnp.where(allowed, scores, -1e30)
            soft_probs = jax.nn.softmax(scores, axis=-1)
            attn_heads = jnp.einsum('ckrl,cle->crke', soft_probs, value_head, preferred_element_type=jnp.float32).astype(jnp.bfloat16)
            attn_heads = attn_heads.reshape(batch_loc, seq_len, attn_width)
            mlp_act = (jax.nn.silu(gate_proj.astype(jnp.float32)) * up_proj.astype(jnp.float32)).astype(jnp.bfloat16)
            group_part = (jnp.dot(attn_heads, w_attn_full, preferred_element_type=jnp.float32) + jnp.dot(mlp_act, w_mlp_full, preferred_element_type=jnp.float32)).astype(jnp.bfloat16)
            z_loc = lax.psum_scatter(group_part, 'model', scatter_dimension=1, tiled=True)
            hidden = (hidden.astype(jnp.float32) + z_loc.astype(jnp.float32)).astype(jnp.bfloat16)
        return hidden

    return jax.shard_map(device_step, mesh=mesh, in_specs=(P(batch_axes, 'model', None), P(batch_axes), P(None, 'data'), P(None, 'data', 'model'), P(None, 'model', 'data'), P(None, 'model', 'data')), out_specs=P(batch_axes, 'model', None), check_vma=False)
```

profile of v0, /device:TPU:97, one launch (start us, length us, event | category | flops | bytes accessed | tf_op | source)
XLA Modules:
  0.0 1596.1 jit_solution(10188621202265872219)
XLA Ops:
  7.9 11.6 all-gather
  27.7 14.9 fusion.83
  42.8 6.2 fusion.84
  53.4 61.5 %all-gather.17.cloned.1.call-done = bf16[2,1024,4096]{2,1,0:T(8,128)(2,1)} async-done(((bf16[2,128,4096]{2,1,0:T(8,128)(2,1)}), bf16[2,1024,4096]{2,1,0:T(8,128)(2,1)}) %all-gather.17.cloned.1.call-update) | async-done | bytes 16777232 | tf_op jit(solution)/shard_map/all_gather | solution.py:42
  115.0 345.9 %all-gather.21.cloned.1.call-done = bf16[1,4096,4864]{2,1,0:T(8,128)(2,1)} async-done(((bf16[1,1024,4864]{2,1,0:T(8,128)(2,1)}), bf16[1,4096,4864]{2,1,0:T(8,128)(2,1)}) %all-gather.21.cloned.1.call-update) | async-done | bytes 39845904 | tf_op jit(solution)/shard_map/all_gather | solution.py:38
  460.9 95.8 %fusion.36 = bf16[2,1024,4864]{2,1,0:T(8,128)(2,1)} fusion(bf16[2,1024,4096]{2,1,0:T(8,128)(2,1)} %all-gather.17.cloned.1.call-done, bf16[1,4096,4864]{2,1,0:T(8,128)(2,1)} %all-gather.21.cloned.1.call-done), kind=kOutput, calls=%fused_computation.46 | convolution fusion | flops 81614340096 | bytes 76546048 | tf_op jit(solution)/shard_map/dot_general | solution.py:43
  556.6 15.3 fusion.10
  572.0 43.3 %all-gather.25.cloned.1.call-done = bf16[1,2048,4096]{2,1,0:T(8,128)(2,1)} async-done(((bf16[1,2048,1024]{2,1,0:T(8,128)(2,1)}), bf16[1,2048,4096]{2,1,0:T(8,128)(2,1)}) %all-gather.25.cloned.1.call-update) | async-done | bytes 16777232 | tf_op jit(solution)/shard_map/all_gather | solution.py:40
  615.3 47.1 %fusion.22 = f32[2,1024,4096]{2,1,0:T(8,128)} fusion(bf16[1,2048,4096]{2,1,0:T(8,128)(2,1)} %all-gather.25.cloned.1.call-done, bf16[2,1024,4864]{2,1,0:T(8,128)(2,1)} %fusion.36), kind=kOutput, calls=%fused_computation.32 | convolution fusion | flops 34393292800 | bytes 67108864 | tf_op jit(solution)/shard_map/dot_general | solution.py:55
  662.4 14.4 fusion.8
  676.8 17.2 %fusion.70 = bf16[2,128,4,1024]{3,1,2,0:T(8,128)(2,1)} fusion(f32[2,1024,1024,4]{2,1,3,0:T(8,128)} %get-tuple-element.16, f32[2,4,1024]{2,1,0:T(4,128)S(1)} %fusion.8, f32[2,4,1024]{2,1,0:T(4,128)S(1)} %get-tuple-element.15, pred[2,1024,1024]{1,2,0:T(8,128)(4,1)S(1)} %copy-done.3, bf16[2,1024,4864]{2,1,0:T(8,128)(2,1)} %fusion.36), kind=kOutput, calls=%fused_computation.84 | convolution fusion | flops 2182086656 | bytes 38338560 | tf_op jit(solution)/shard_map/ckrl,cle->crke/dot_general | solution.py:52
  694.0 23.6 %add_convert_fusion.1 = bf16[2,1024,4096]{2,1,0:T(8,128)(2,1)} fusion(f32[2,1024,4096]{2,1,0:T(8,128)} %fusion.22, bf16[2,1024,512]{1,2,0:T(8,128)(2,1)} %bitcast.107, bf16[1,512,4096]{2,1,0:T(8,128)(2,1)} %all-gather.23.cloned.1.call-done), kind=kOutput, calls=%fused_computation.8 | convolution fusion | flops 8606711808 | bytes 56623104 | tf_op jit(solution)/shard_map/dot_general | solution.py:55
  718.4 9.0 all-gather.4
  727.4 80.4 %reduce-scatter.3.cloned.1.call-done = bf16[2,128,4096]{2,1,0:T(8,128)(2,1)} async-done(((bf16[2,1024,4096]{2,1,0:T(8,128)(2,1)}), bf16[2,128,4096]{2,1,0:T(8,128)(2,1)}) %reduce-scatter.3.cloned.1.call-update) | async-done | bytes 2097168 | tf_op jit(solution)/shard_map/reduce_scatter | solution.py:56
  815.5 338.1 %all-gather.27.cloned.1.call-done = bf16[1,4096,4864]{2,1,0:T(8,128)(2,1)} async-done(((bf16[1,1024,4864]{2,1,0:T(8,128)(2,1)}), bf16[1,4096,4864]{2,1,0:T(8,128)(2,1)}) %all-gather.27.cloned.1.call-update) | async-done | bytes 39845904 | tf_op jit(solution)/shard_map/all_gather | solution.py:38
  1153.6 85.3 %all-gather.19.cloned.1.call-done = bf16[2,1024,4096]{2,1,0:T(8,128)(2,1)} async-done(((bf16[2,128,4096]{2,1,0:T(8,128)(2,1)}), bf16[2,1024,4096]{2,1,0:T(8,128)(2,1)}) %all-gather.19.cloned.1.call-update) | async-done | bytes 16777232 | tf_op jit(solution)/shard_map/all_gather | solution.py:42
  1238.9 95.9 %fusion.39 = bf16[2,1024,4864]{2,1,0:T(8,128)(2,1)} fusion(bf16[2,1024,4096]{2,1,0:T(8,128)(2,1)} %all-gather.19.cloned.1.call-done, bf16[1,4096,4864]{2,1,0:T(8,128)(2,1)} %all-gather.27.cloned.1.call-done), kind=kOutput, calls=%fused_computation.47 | convolution fusion | flops 81614340096 | bytes 76546048 | tf_op jit(solution)/shard_map/dot_general | solution.py:43
  1334.8 15.3 fusion.11
  1350.1 42.6 %all-gather.31.cloned.1.call-done = bf16[1,2048,4096]{2,1,0:T(8,128)(2,1)} async-done(((bf16[1,2048,1024]{2,1,0:T(8,128)(2,1)}), bf16[1,2048,4096]{2,1,0:T(8,128)(2,1)}) %all-gather.31.cloned.1.call-update) | async-done | bytes 16777232 | tf_op jit(solution)/shard_map/all_gather | solution.py:40
  1392.8 47.1 %fusion.20 = f32[2,1024,4096]{2,1,0:T(8,128)} fusion(bf16[1,2048,4096]{2,1,0:T(8,128)(2,1)} %all-gather.31.cloned.1.call-done, bf16[2,1024,4864]{2,1,0:T(8,128)(2,1)} %fusion.39), kind=kOutput, calls=%fused_computation.30 | convolution fusion | flops 34393292800 | bytes 67108864 | tf_op jit(solution)/shard_map/dot_general | solution.py:55
  1439.9 14.4 fusion.9
  1454.3 17.2 %fusion.73 = bf16[2,128,4,1024]{3,1,2,0:T(8,128)(2,1)} fusion(f32[2,1024,1024,4]{2,1,3,0:T(8,128)} %get-tuple-element.18, f32[2,4,1024]{2,1,0:T(4,128)S(1)} %fusion.9, f32[2,4,1024]{2,1,0:T(4,128)S(1)} %get-tuple-element.17, pred[2,1024,1024]{1,2,0:T(8,128)(4,1)S(1)} %copy-done.4, bf16[2,1024,4864]{2,1,0:T(8,128)(2,1)} %fusion.39), kind=kOutput, calls=%fused_computation.85 | convolution fusion | flops 2182086656 | bytes 38338560 | tf_op jit(solution)/shard_map/ckrl,cle->crke/dot_general | solution.py:52
  1471.5 23.5 %add_convert_fusion = bf16[2,1024,4096]{2,1,0:T(8,128)(2,1)} fusion(f32[2,1024,4096]{2,1,0:T(8,128)} %fusion.20, bf16[2,1024,512]{1,2,0:T(8,128)(2,1)} %bitcast.106, bf16[1,512,4096]{2,1,0:T(8,128)(2,1)} %all-gather.29.cloned.1.call-done), kind=kOutput, calls=%fused_computation.6 | convolution fusion | flops 8606711808 | bytes 56623104 | tf_op jit(solution)/shard_map/dot_general | solution.py:55
  1495.1 90.1 %reduce-scatter.5.cloned.1.call-done = bf16[2,128,4096]{2,1,0:T(8,128)(2,1)} async-done(((bf16[2,1024,4096]{2,1,0:T(8,128)(2,1)}), bf16[2,128,4096]{2,1,0:T(8,128)(2,1)}) %reduce-scatter.5.cloned.1.call-update) | async-done | bytes 2097168 | tf_op jit(solution)/shard_map/reduce_scatter | solution.py:56
  (56 shorter events, 26.2 us)
Async XLA Ops:
  6.5 108.4 %all-gather.17.cloned.1.call-start = ((), (), s32[]{:S(2)}) async-start(), calls=%async_computation.2 | async-start | bytes 18874368 | tf_op jit(solution)/shard_map/all_gather | solution.py:42
  27.6 433.3 %all-gather.21.cloned.1.call-start = ((), (), s32[]{:S(2)}) async-start(), calls=%async_computation.6 | async-start | bytes 49807360 | tf_op jit(solution)/shard_map/all_gather | solution.py:38
  42.6 6.4 copy-start.5
  42.6 8.6 copy-start.7
  42.7 572.6 %all-gather.25.cloned.1.call-start = ((), (), s32[]{:S(2)}) async-start(), calls=%async_computation.8 | async-start | bytes 20971520 | tf_op jit(solution)/shard_map/all_gather | solution.py:40
  49.0 645.0 %all-gather.23.cloned.1.call-start = ((), (), s32[]{:S(2)}) async-start(), calls=%async_computation.7 | async-start | bytes 5242880 | tf_op jit(solution)/shard_map/all_gather | solution.py:39
  50.6 757.2 %reduce-scatter.3.cloned.1.call-start = ((), (), s32[]{:S(2)}) async-start(), calls=%async_computation.3 | async-start | bytes 18874368 | tf_op jit(solution)/shard_map/reduce_scatter | solution.py:56
  460.9 95.8 %copy-start.3 = (pred[2,1024,1024]{1,2,0:T(8,128)(4,1)S(1)}, pred[2,1024,1024]{1,2,0:T(8,128)(4,1)}, u32[]{:S(2)}) copy-start(pred[2,1024,1024]{1,2,0:T(8,128)(4,1)} %broadcast_and_fusion) | copy-start | bytes 6291460
  717.6 0.8 copy-start.6
  717.6 90.2 %copy-start.2 = (bf16[2,128,4096]{2,1,0:T(8,128)(2,1)S(1)}, bf16[2,128,4096]{2,1,0:T(8,128)(2,1)}, u32[]{:S(2)}) copy-start(bf16[2,128,4096]{2,1,0:T(8,128)(2,1)} %param.6) | copy-start | bytes 6291460
  717.7 435.9 %all-gather.27.cloned.1.call-start = ((), (), s32[]{:S(2)}) async-start(), calls=%async_computation.9 | async-start | bytes 49807360 | tf_op jit(solution)/shard_map/all_gather | solution.py:38
  718.3 520.6 %all-gather.19.cloned.1.call-start = ((), (), s32[]{:S(2)}) async-start(), calls=%async_computation.4 | async-start | bytes 18874368 | tf_op jit(solution)/shard_map/all_gather | solution.py:42
  810.3 1.3 copy-start
  813.8 578.9 %all-gather.31.cloned.1.call-start = ((), (), s32[]{:S(2)}) async-start(), calls=%async_computation.11 | async-start | bytes 20971520 | tf_op jit(solution)/shard_map/all_gather | solution.py:40
  814.6 656.9 %all-gather.29.cloned.1.call-start = ((), (), s32[]{:S(2)}) async-start(), calls=%async_computation.10 | async-start | bytes 5242880 | tf_op jit(solution)/shard_map/all_gather | solution.py:39
  815.4 769.8 %reduce-scatter.5.cloned.1.call-start = ((), (), s32[]{:S(2)}) async-start(), calls=%async_computation.5 | async-start | bytes 18874368 | tf_op jit(solution)/shard_map/reduce_scatter | solution.py:56
  1238.9 95.9 %copy-start.4 = (pred[2,1024,1024]{1,2,0:T(8,128)(4,1)S(1)}, pred[2,1024,1024]{1,2,0:T(8,128)(4,1)}, u32[]{:S(2)}) copy-start(pred[2,1024,1024]{1,2,0:T(8,128)(4,1)} %broadcast_and_fusion) | copy-start | bytes 6291460
  1495.0 90.2 %copy-start.1 = (bf16[2,128,4096]{2,1,0:T(8,128)(2,1)S(1)}, bf16[2,128,4096]{2,1,0:T(8,128)(2,1)}, u32[]{:S(2)}) copy-start(bf16[2,128,4096]{2,1,0:T(8,128)(2,1)} %copy-done) | copy-start | bytes 6291460
Sparse Core Ops, SparseCore 0:
  27.7 87.1 all-gather.16
  116.5 344.2 all-gather.20
  462.4 152.8 all-gather.24
  616.7 46.4 all-gather.22
  717.8 90.0 reduce-scatter.2
  809.3 344.2 all-gather.26
  1155.2 83.6 all-gather.18
  1240.5 152.2 all-gather.30
  1394.3 46.4 all-gather.28
  1495.2 89.9 reduce-scatter.4
where the time goes:
time: 1600 us
  waiting for transfers between devices  1090 us (68%)
  matrix products  398 us (25%)
  other arithmetic  48.3 us (3%)
  local copies, waits for them, and re-layouts  24.6 us (2%)
  blocking collectives  20.6 us (1%)
    all_gather x2, waiting for transfers between devices, device_step(): w_in_full = lax.all_gather(w_in_loc[layer_idx], 'data', axis=0, tiled=True)  684 us
    dot_general x2, matrix products, device_step(): jnp.dot(h_full, w_in_full, preferred_element_type=jnp.float32)  192 us
    reduce_scatter x2, waiting for transfers between devices, device_step(): lax.psum_scatter(group_part, 'model', scatter_dimension=1, tiled=True)  171 us
    all_gather x2, waiting for transfers between devices, device_step(): h_full = lax.all_gather(normed, 'model', axis=1, tiled=True)  147 us
    dot_general x2, matrix products, device_step(): jnp.dot(mlp_act, w_mlp_full, preferred_element_type=jnp.float32)  94.3 us
    all_gather x2, waiting for transfers between devices, device_step(): lax.all_gather(w_mlp_loc[layer_idx], 'data', axis=1, tiled=True)  86 us
    dot_general x2, matrix products, device_step(): jnp.dot(attn_heads, w_attn_full, preferred_element_type=jnp.float32)  47.1 us
    dot_general x2, matrix products, device_step(): jnp.einsum('ckrl,cle->crke', soft_probs, value_head, preferred_element_ty...  34.4 us
  transfers between devices with their start and end apart: 10, of which 8 were waited for; matrix products, arithmetic and copies ran while one was open for 26% of the time, Pallas kernels for 0%

commit v1 on v0

v1 whole, which is shorter than its diff:
```python
import functools

import jax
import jax.numpy as jnp
from jax import lax
from jax.experimental import pallas as pl
from jax.experimental.pallas import tpu as pltpu
from jax.sharding import PartitionSpec as P

EPSILON = 1e-6
NEG_BIG = -1e30
MESH = pl.DeviceIdType.MESH
BF = jnp.bfloat16
F32 = jnp.float32
NS = 3


def kernel(cfg, x_ref, kl_ref, gain_ref, wi_ref, wa_ref, wm_ref,
           y_ref, wi_buf, wa_buf, wm_buf,
           hv, qkv, om, wv, zs, ra, rb, cst, parts, xv, hs, gfull, klb, kcur,
           w_r1, w_r2, w_d1, w_d2, w_s1, w_s2, w_s3, w_s4, wld, misc,
           g_s, g_r, k_s, k_r, ax_s, ax_r, ad_s, ad_r, rg_s, rg_r, rf_s, rf_r,
           a_s, a_r, b_s, b_r, c_s, pd_r, pa_r, free_sem):
    (n_data, n_x, nb, sl, dm, dloc, qw, hd, ff, nl) = cfg
    seq = sl * 2 * n_x
    blk = 2 * sl
    cw = 512
    hw = cw // 2
    kv0 = qw
    ff0 = qw + 2 * hd
    n_gu = ff // hw
    n_in = 2 + n_gu
    n_out = dloc // cw
    n_u = n_in + n_out
    n_t = n_data * n_out
    rw = qw + ff

    d = lax.axis_index('data')
    m = lax.axis_index('model')
    x = lax.div(m, 2)
    c = lax.rem(m, 2)
    d_odd = lax.rem(d, 2)
    nbr1 = d + 1 - 2 * d_odd
    nbr3 = n_data - 1 - d
    opp = lax.rem(d + 2, n_data)
    xr = lax.rem(x + 1, n_x)
    xl = lax.rem(x + n_x - 1, n_x)
    xo = lax.rem(x + 2, n_x)

    def dev(dd, xx, cc):
        return {'data': dd, 'model': xx * 2 + cc}

    def rc(src, dst, ss, rs, to):
        return pltpu.make_async_remote_copy(src_ref=src, dst_ref=dst, send_sem=ss, recv_sem=rs, device_id=to, device_id_type=MESH)

    other = dev(d, x, 1 - c)
    right = dev(d, xr, c)
    left = dev(d, xl, c)

    class Lay:
        pass

    lays = []
    for l in range(nl):
        L = Lay()
        L.l = l
        if l % 2 == 0:
            L.p, L.q, a = nbr1, nbr3, lax.div(d, 2)
        else:
            L.p, L.q, a = nbr3, nbr1, lax.rem(lax.div(d + 1, 2), 2)
        L.isb = (c - a) * (c - a)
        L.src1 = L.p + (L.q - L.p) * L.isb
        L.srcx = L.q + (L.p - L.q) * L.isb
        L.src2 = opp + (d - opp) * L.isb
        L.first = dev(L.src1, x, c + (1 - 2 * c) * L.isb)
        L.pair = dev(L.p, x, c)
        lays.append(L)

    barrier = pltpu.get_barrier_semaphore()
    friends = [other, right, left, dev(nbr1, x, 0), dev(nbr1, x, 1), dev(nbr3, x, 0), dev(nbr3, x, 1), dev(opp, x, c)]
    for f in friends:
        pl.semaphore_signal(barrier, inc=1, device_id=f, device_id_type=MESH)
    xload = pltpu.make_async_copy(x_ref, xv, misc.at[0])
    xload.start()
    pl.semaphore_wait(barrier, len(friends))

    def cols(start, width):
        return pl.ds(start if isinstance(start, int) else pl.multiple_of(start, 128), width)

    class Unit:
        def __init__(self, L, s, parts_):
            self.L, self.idx, self.parts = L, (L.l * n_u + s) * 2, parts_

    def unit_in(L, s):
        l = L.l
        if isinstance(s, int) and s == 0:
            spans = [(0, qw)]
        elif isinstance(s, int) and s == 1:
            spans = [(kv0, 2 * hd)]
        else:
            k = s - 2
            spans = [(ff0 + hw * k, hw), (ff0 + ff + hw * k, hw)]
        return Unit(L, s, [(wi_ref.at[l, :, cols(c0, w)], functools.partial(lambda c0, w, e: wi_buf.at[l, e, :, cols(c0, w)], c0, w))
                           for c0, w in spans])

    def unit_out(L, v):
        l = L.l
        cc = cols(v * cw, cw)
        return Unit(L, n_in + v, [(wa_ref.at[l, :, cc], lambda e: wa_buf.at[l, e, :, cc]), (wm_ref.at[l, :, cc], lambda e: wm_buf.at[l, e, :, cc])])

    def send_own(u, cond=None):
        L = u.L

        def go():
            for i, (own, buf) in enumerate(u.parts):
                rc(own, buf(d), w_s1.at[u.idx + i], w_r1.at[u.idx + i], L.first).start()

        def go2():
            for i, (own, buf) in enumerate(u.parts):
                rc(own, buf(d), w_s3.at[u.idx + i], w_d2.at[u.idx + i], other).start()

        if cond is None or cond == 'a':
            @pl.when(L.isb == 0)
            def _():
                go2()
        if cond is None:
            go()
        else:
            @pl.when(L.isb == (0 if cond == 'a' else 1))
            def _():
                go()

    def fwd1(u):
        L = u.L
        for i, (own, buf) in enumerate(u.parts):
            rc(own, buf(L.src1), w_s1.at[u.idx + i], w_r1.at[u.idx + i], L.first).wait_recv()
            rc(buf(L.src1), buf(L.src1), w_s2.at[u.idx + i], w_d1.at[u.idx + i], other).start()

            @pl.when(L.isb == 1)
            def _():
                rc(buf(L.src1), buf(L.src1), w_s4.at[u.idx + i], w_r2.at[u.idx + i], L.pair).start()

    def fwd2(u):
        L = u.L

        @pl.when(L.isb == 1)
        def _():
            for i, (own, buf) in enumerate(u.parts):
                rc(own, buf(opp), w_s4.at[u.idx + i], w_r2.at[u.idx + i], L.pair).wait_recv()
                rc(buf(opp), buf(opp), w_s3.at[u.idx + i], w_d2.at[u.idx + i], other).start()

    def got1(u):
        for i, (own, buf) in enumerate(u.parts):
            rc(own, buf(u.L.srcx), w_s2.at[u.idx + i], w_d1.at[u.idx + i], other).wait_recv()

    def got2(u):
        for i, (own, buf) in enumerate(u.parts):
            rc(own, buf(u.L.src2), w_s3.at[u.idx + i], w_d2.at[u.idx + i], other).wait_recv()

    def sends_done(u):
        L = u.L
        for i, (own, buf) in enumerate(u.parts):
            rc(own, buf(d), w_s1.at[u.idx + i], w_r1.at[u.idx + i], L.first).wait_send()
            rc(own, buf(d), w_s2.at[u.idx + i], w_d1.at[u.idx + i], other).wait_send()
            rc(own, buf(d), w_s3.at[u.idx + i], w_d2.at[u.idx + i], other).wait_send()

            @pl.when(L.isb == 1)
            def _():
                rc(own, buf(d), w_s4.at[u.idx + i], w_r2.at[u.idx + i], L.pair).wait_send()

    def load_in(u, slot):
        L = u.L
        off = 0
        for own, buf in u.parts:
            w = own.shape[-1]

            def to(e):
                return wv.at[slot, pl.ds(pl.multiple_of(e * dloc, dloc), dloc), pl.ds(off, w)]

            for e in (L.p, L.q, opp):
                pltpu.make_async_copy(buf(e), to(e), wld.at[slot]).start()

            @pl.when(L.isb == 0)
            def _():
                pltpu.make_async_copy(own, to(d), wld.at[slot]).start()

            @pl.when(L.isb == 1)
            def _():
                pltpu.make_async_copy(buf(d), to(d), wld.at[slot]).start()
            off += w

    def wait_in(slot, w):
        pltpu.make_async_copy(wv.at[slot, :, pl.ds(0, w)], wv.at[slot, :, pl.ds(0, w)], wld.at[slot]).wait()

    def z_src(L, t):
        k, v = lax.div(t, n_out), lax.rem(t, n_out)
        src = jnp.where(k == 0, d, jnp.where(k == 1, L.q, jnp.where(k == 2, L.p, opp)))
        return k, v, src

    def z_col(L, t):
        _, v, src = z_src(L, t)
        return src * n_out + v

    def load_out(L, t, slot):
        k, v, src = z_src(L, t)
        u = unit_out(L, v)
        spots = (wv.at[slot, pl.ds(0, qw), :], wv.at[slot, pl.ds(qw, ff), :])
        mine = jnp.logical_and(k == 0, L.isb == 0)

        @pl.when(mine)
        def _():
            for (own, buf), to in zip(u.parts, spots):
                pltpu.make_async_copy(own, to, wld.at[slot]).start()

        @pl.when(jnp.logical_not(mine))
        def _():
            for (own, buf), to in zip(u.parts, spots):
                pltpu.make_async_copy(buf(src), to, wld.at[slot]).start()

    def wait_out(slot):
        ref = wv.at[slot, pl.ds(0, rw), :]
        pltpu.make_async_copy(ref, ref, wld.at[slot]).wait()

    def out_arrives(L, t):
        k, v, src = z_src(L, t)
        u = unit_out(L, v)

        @pl.when(jnp.logical_and(k == 0, L.isb == 1))
        def _():
            got2(u)

        @pl.when(jnp.logical_and(k == 1, L.isb == 0))
        def _():
            got1(u)

        @pl.when(jnp.logical_and(k == 2, L.isb == 0))
        def _():
            fwd1(u)

        @pl.when(jnp.logical_and(k == 2, L.isb == 1))
        def _():
            got1(u)

        @pl.when(k == 3)
        def _():
            fwd2(u)

        @pl.when(jnp.logical_and(k == 3, L.isb == 0))
        def _():
            got2(u)

    rows = 32

    def layer_norm(L, b):
        g = gfull[L.l, 0:1, :]

        def tile(i, _):
            r = pl.ds(pl.multiple_of(i * rows, rows), rows)
            v = xv[b, r, :].astype(F32)
            cen = v - jnp.mean(v, axis=-1, keepdims=True)
            var = jnp.mean(cen * cen, axis=-1, keepdims=True)
            h = (cen * lax.rsqrt(var + EPSILON) * g).astype(BF)
            hs[b, r, :] = h

            @pl.when(c == 0)
            def _():
                hv[b, pl.ds(pl.multiple_of(m * sl + i * rows, rows), rows), :] = h
            return 0

        lax.fori_loop(0, sl // rows, tile, 0)

    def my_rows(b):
        return hv.at[b, pl.ds(pl.multiple_of(m * sl, sl), sl), :]

    def block(b, xx, lo=0, n=None):
        return hv.at[b, pl.ds(pl.multiple_of(xx * blk, blk), blk), pl.ds(lo, dm if n is None else n)]

    def ax(L, b):
        i = L.l * nb + b
        return rc(hs.at[b], my_rows(b), ax_s.at[i], ax_r.at[2 * i + c], dev(L.q, x, 1))

    def ad(L, b):
        i = L.l * nb + b
        return rc(hs.at[b], my_rows(b), ad_s.at[i], ad_r.at[i], other)

    def share(L, b):
        ax(L, b).start()

        @pl.when(c == 1)
        def _():
            ad(L, b).start()

    def ring(L, b, way):
        i = 2 * (L.l * nb + b) + way
        return rc(block(b, x), block(b, x), rg_s.at[i], rg_r.at[i], right if way == 0 else left)

    def ring_in(L, b, way):
        i = 2 * (L.l * nb + b) + way
        src = block(b, xl if way == 0 else xr)
        return rc(src, src, rg_s.at[i], rg_r.at[i], right if way == 0 else left)

    def ring2(L, b, way, xx):
        i = 2 * (L.l * nb + b) + way
        src = block(b, xx, 0 if way == 0 else dm // 2, dm // 2)
        return rc(src, src, rf_s.at[i], rf_r.at[i], right if way == 0 else left)

    def ring_start(L, b):
        i = L.l * nb + b

        @pl.when(c == 0)
        def _():
            dst = hv.at[b, pl.ds(pl.multiple_of(x * blk + sl, sl), sl), :]
            rc(hs.at[b], dst, ad_s.at[i], ad_r.at[i], other).wait_recv()

        @pl.when(c == 1)
        def _():
            for cc in range(2):
                dst = hv.at[b, pl.ds(pl.multiple_of(x * blk + cc * sl, sl), sl), :]
                rc(hs.at[b], dst, ax_s.at[i], ax_r.at[2 * i + cc], other).wait_recv()
        for way in range(2):
            ring(L, b, way).start()

    def ring_pass(L, b):
        for way in range(2):
            ring_in(L, b, way).wait_recv()
            ring2(L, b, way, xl if way == 0 else xr).start()

    def ring_end(L, b):
        for way in range(2):
            ring2(L, b, way, xo).wait_recv()

    def gather_sends_done(L, b):
        ax(L, b).wait_send()

        @pl.when(c == 1)
        def _():
            ad(L, b).wait_send()
        for way in range(2):
            ring(L, b, way).wait_send()
            ring2(L, b, way, xl if way == 0 else xr).wait_send()

    def p_q(b, slot):
        qkv[b, :, 0:qw] = jnp.dot(hv[b], wv[slot], preferred_element_type=F32).astype(BF)

    def p_kv(b, slot):
        qkv[b, :, qw:qw + 2 * hd] = jnp.dot(hv[b], wv[slot, :, 0:2 * hd], preferred_element_type=F32).astype(BF)

    def p_gu(b, slot, k):
        acc = jnp.dot(hv[b], wv[slot], preferred_element_type=F32)
        g = acc[:, 0:hw].astype(BF).astype(F32)
        up = acc[:, hw:cw].astype(BF).astype(F32)
        om[b, :, cols(qw + hw * k, hw)] = (g * (1.0 / (1.0 + jnp.exp(-g))) * up).astype(BF)

    def attention(b):
        tq = 256
        kl = kcur[b, 0:1, 0:1]
        for i in range(seq // tq):
            n = tq * (i + 1)
            row = lax.broadcasted_iota(jnp.int32, (tq, n), 0) + tq * i
            col = lax.broadcasted_iota(jnp.int32, (tq, n), 1)
            ok = jnp.logical_and(col <= row, col < kl)

            def head(h, _):
                hc = pl.ds(pl.multiple_of(h * hd, hd), hd)
                qh = qkv[b, tq * i:tq * (i + 1), hc]
                s = lax.dot_general(qh, qkv[b, 0:n, kv0:kv0 + hd], (((1,), (1,)), ((), ())), preferred_element_type=F32) * hd ** -0.5
                s = jnp.where(ok, s, NEG_BIG)
                e = jnp.exp(s - jnp.max(s, axis=-1, keepdims=True))
                tot = jnp.sum(e, axis=-1, keepdims=True)
                o = jnp.dot(e.astype(BF), qkv[b, 0:n, kv0 + hd:kv0 + 2 * hd], preferred_element_type=F32)
                om[b, tq * i:tq * (i + 1), hc] = (o / tot).astype(BF)
                return 0

            lax.fori_loop(0, qw // hd, head, 0)

    def zblk(slot, xx, lo, n):
        return zs.at[slot, pl.ds(pl.multiple_of(xx * blk, blk), blk), pl.ds(lo, n)]

    def a_send(slot, way):
        return rc(zblk(slot, xo, way * hw, hw), ra.at[slot, way], a_s.at[2 * slot + way], a_r.at[2 * slot + way], right if way == 0 else left)

    def b_send(slot, way):
        return rc(zblk(slot, xr if way == 0 else xl, 0, cw), rb.at[slot, way], b_s.at[2 * slot + way], b_r.at[2 * slot + way],
                  right if way == 0 else left)

    def z_step(b, wslot, j):
        slot = lax.rem(j, NS)

        @pl.when(j >= NS)
        def _():
            for way in range(2):
                a_send(slot, way).wait_send()
                b_send(slot, way).wait_send()
        zs[slot] = jnp.dot(om[b], wv[wslot, 0:rw, :], preferred_element_type=F32).astype(BF)
        for way in range(2):
            a_send(slot, way).start()

    def rs_b(j):
        slot = lax.rem(j, NS)
        for way in range(2):
            a_send(slot, way).wait_recv()
            r = pl.ds(pl.multiple_of((xr if way == 0 else xl) * blk, blk), blk)
            cc = pl.ds(way * hw, hw)
            zs[slot, r, cc] = (zs[slot, r, cc].astype(F32) + ra[slot, way].astype(F32)).astype(BF)
        for way in range(2):
            b_send(slot, way).start()

    def c_send(L, b, n, slot, cc, home):
        i = (L.l * n_t + n) * nb + b
        sem = c_s.at[2 * slot + cc]
        if home:
            return rc(cst.at[slot, pl.ds(cc * sl, sl), :], parts.at[0, b, :, cols(n * cw, cw)], sem, pd_r.at[i], other)
        return rc(cst.at[slot, pl.ds(cc * sl, sl), :], parts.at[1, b, :, cols(n * cw, cw)], sem, pa_r.at[i], dev(L.q, x, cc))

    def c_wait(L, slot):
        @pl.when(c == 1)
        def _():
            for cc in range(2):
                c_send(L, 0, 0, slot, cc, False).wait_send()

        @pl.when(c == 0)
        def _():
            c_send(L, 0, 0, slot, 1, True).wait_send()

    def rs_c(L, j, b, t):
        slot = lax.rem(j, NS)
        n = z_col(L, t)
        for way in range(2):
            b_send(slot, way).wait_recv()

        @pl.when(j >= NS)
        def _():
            c_wait(L, slot)
        r = pl.ds(pl.multiple_of(x * blk, blk), blk)
        cst[slot] = (zs[slot, r, :].astype(F32) + rb[slot, 0].astype(F32) + rb[slot, 1].astype(F32)).astype(BF)

        @pl.when(c == 0)
        def _():
            c_send(L, b, n, slot, 1, True).start()
            parts[0, b, :, cols(n * cw, cw)] = cst[slot, 0:sl, :]

        @pl.when(c == 1)
        def _():
            for cc in range(2):
                c_send(L, b, n, slot, cc, False).start()

    def combine(L, b):
        for n in range(n_t):
            c_send(L, b, n, 0, 0, False).wait_recv()

            @pl.when(c == 1)
            def _():
                c_send(L, b, n, 0, 0, True).wait_recv()

        def tile(i, _):
            r = pl.ds(pl.multiple_of(i * rows, rows), rows)
            z = parts[0, b, r, :].astype(F32) + parts[1, b, r, :].astype(F32)
            xv[b, r, :] = (xv[b, r, :].astype(F32) + z).astype(BF)
            return 0

        lax.fori_loop(0, sl // rows, tile, 0)

    L0, L1 = lays
    send_own(unit_in(L0, 0))
    send_own(unit_in(L0, 1))
    g_to = [dev(nbr1, x, c), dev(nbr3, x, c), dev(opp, x, c)]

    def gsl(e):
        return gfull.at[:, :, pl.ds(pl.multiple_of(e * dloc, dloc), dloc)]

    for i in range(3):
        rc(gain_ref, gsl(d), g_s.at[i], g_r.at[i], g_to[i]).start()

    @pl.when(c == 1)
    def _():
        for l, L in enumerate(lays):
            rc(kl_ref, klb.at[l], k_s.at[l], k_r.at[l], dev(L.q, x, 1)).start()
    gfull[:, :, pl.ds(pl.multiple_of(d * dloc, dloc), dloc)] = gain_ref[...]

    def set_len(L):
        @pl.when(c == 0)
        def _():
            kcur[...] = kl_ref[...]

        @pl.when(c == 1)
        def _():
            rc(kl_ref, klb.at[L.l], k_s.at[L.l], k_r.at[L.l], other).wait_recv()
            kcur[...] = klb[L.l]

    set_len(L0)
    xload.wait()
    for i, e in enumerate((nbr1, nbr3, opp)):
        rc(gain_ref, gsl(e), g_s.at[i], g_r.at[i], g_to[i]).wait_recv()
    for b in range(nb):
        layer_norm(L0, b)
        share(L0, b)
    for s in range(2, n_in):
        send_own(unit_in(L0, s))
    for v in range(n_out):
        send_own(unit_out(L0, v))
    for b in range(nb):
        ring_start(L0, b)
    for s in range(3):
        fwd1(unit_in(L0, s))
    for b in range(nb):
        ring_pass(L0, b)

    def in_ready(L, s):
        u = unit_in(L, s)
        fwd2(u)
        got1(u)
        got2(u)

    for s in range(1):
        in_ready(L0, s)
        load_in(unit_in(L0, s), 0)
    for b in range(nb):
        ring_end(L0, b)

    def both(fn):
        def body(b, _):
            fn(b)
            return 0
        lax.fori_loop(0, nb, body, 0)

    fwd1(unit_in(L0, 3))
    in_ready(L0, 1)
    load_in(unit_in(L0, 1), 1)
    wait_in(0, cw)
    both(lambda b: p_q(b, 0))
    fwd1(unit_in(L0, 4))
    in_ready(L0, 2)
    load_in(unit_in(L0, 2), 0)
    wait_in(1, 2 * hd)
    both(lambda b: p_kv(b, 1))
    both(attention)

    def gu_loop0(k, _):
        s = k + 2
        slot = lax.rem(k, 2)

        @pl.when(s + 3 < n_in)
        def _():
            fwd1(unit_in(L0, s + 3))

        @pl.when(jnp.logical_and(jnp.logical_and(s + 3 >= n_in, s + 3 < n_u), L0.isb == 1))
        def _():
            fwd1(unit_out(L0, s + 3 - n_in))

        @pl.when(s + 1 < n_in)
        def _():
            in_ready(L0, s + 1)
            load_in(unit_in(L0, s + 1), 1 - slot)

        @pl.when(s + 1 == n_in)
        def _():
            out_arrives(L0, 0)
            load_out(L0, 0, 1 - slot)
        wait_in(slot, cw)
        both(lambda b: p_gu(b, slot, k))

        @pl.when(k >= n_gu // 2)
        def _():
            u = k - n_gu // 2

            @pl.when(u >= 2)
            def _():
                send_own(unit_in(L1, u), 'a')
        return 0

    lax.fori_loop(0, n_gu, gu_loop0, 0)
    send_own(unit_in(L1, 0), 'a')
    send_own(unit_in(L1, 1), 'a')
    for b in range(nb):
        gather_sends_done(L0, b)
    @pl.when(c == 1)
    def _():
        for cc in range(2):
            pl.semaphore_signal(free_sem, inc=1, device_id=dev(L1.q, x, cc), device_id_type=MESH)
    z0 = lax.rem(n_gu, 2)

    def z_loop0(t, _):
        wslot = lax.rem(t + z0, 2)
        wait_out(wslot)
        for b in range(nb):
            j = nb * t + b
            z_step(b, wslot, j)

            @pl.when(j >= 1)
            def _():
                rs_b(j - 1)

            @pl.when(j >= 2)
            def _():
                rs_c(L0, j - 2, b, t - 1)
            if b == 0:
                @pl.when(t + 1 < n_t)
                def _():
                    out_arrives(L0, t + 1)
                    load_out(L0, t + 1, 1 - wslot)

                @pl.when(t + 4 < n_in)
                def _():
                    send_own(unit_in(L1, t + 4), 'a')
        return 0

    lax.fori_loop(0, n_t, z_loop0, 0)
    j_end = nb * n_t
    for s in range(2):
        send_own(unit_in(L1, s), 'b')
    rs_b(j_end - 1)
    rs_c(L0, j_end - 2, 0, n_t - 1)
    rs_c(L0, j_end - 1, 1, n_t - 1)

    def layer_sends_done(L):
        sends_done(unit_in(L, 0))
        sends_done(unit_in(L, 1))

        def body(s, _):
            sends_done(unit_in(L, s))
            return 0
        lax.fori_loop(2, n_in, body, 0)

        def body2(v, _):
            sends_done(unit_out(L, v))
            return 0
        lax.fori_loop(0, n_out, body2, 0)

    pl.semaphore_wait(free_sem, 1)
    for b in range(nb):
        combine(L0, b)
        layer_norm(L1, b)
        share(L1, b)
    set_len(L1)
    for s in range(2, n_in):
        send_own(unit_in(L1, s), 'b')
    for v in range(n_out):
        send_own(unit_out(L1, v))
    ring_start(L1, 0)
    fwd1(unit_in(L1, 0))
    fwd1(unit_in(L1, 1))
    ring_start(L1, 1)
    fwd1(unit_in(L1, 2))
    ring_pass(L1, 0)
    fwd1(unit_in(L1, 3))
    in_ready(L1, 0)
    load_in(unit_in(L1, 0), 0)
    in_ready(L1, 1)
    load_in(unit_in(L1, 1), 1)
    ring_end(L1, 0)
    wait_in(0, cw)
    p_q(0, 0)
    fwd1(unit_in(L1, 4))
    in_ready(L1, 2)
    load_in(unit_in(L1, 2), 0)
    wait_in(1, 2 * hd)
    p_kv(0, 1)
    ring_pass(L1, 1)
    attention(0)

    def gu_loop1(k, _):
        s = k + 2
        slot = lax.rem(k, 2)

        @pl.when(s + 3 < n_in)
        def _():
            fwd1(unit_in(L1, s + 3))

        @pl.when(jnp.logical_and(jnp.logical_and(s + 3 >= n_in, s + 3 < n_u), L1.isb == 1))
        def _():
            fwd1(unit_out(L1, s + 3 - n_in))

        @pl.when(s + 1 < n_in)
        def _():
            in_ready(L1, s + 1)
            load_in(unit_in(L1, s + 1), 1 - slot)
        wait_in(slot, cw)
        p_gu(0, slot, k)
        return 0

    lax.fori_loop(0, n_gu, gu_loop1, 0)
    load_in(unit_in(L1, 0), 0)
    load_in(unit_in(L1, 1), 1)
    ring_end(L1, 1)
    wait_in(0, cw)
    p_q(1, 0)
    load_in(unit_in(L1, 2), 0)
    wait_in(1, 2 * hd)
    p_kv(1, 1)
    out_arrives(L1, 0)
    load_out(L1, 0, 1)
    attention(1)

    def fused(k, _):
        wait_in(0, cw)
        p_gu(1, 0, k)

        @pl.when(k + 1 < n_gu)
        def _():
            load_in(unit_in(L1, k + 3), 0)

        @pl.when(k + 1 == n_gu)
        def _():
            load_out(L1, 0, 0)
        wait_out(1)
        j = j_end + k
        z_step(0, 1, j)

        @pl.when(k >= 1)
        def _():
            rs_b(j - 1)

        @pl.when(k >= 2)
        def _():
            rs_c(L1, j - 2, 0, k - 2)

        @pl.when(k + 1 < n_t)
        def _():
            out_arrives(L1, k + 1)
            load_out(L1, k + 1, 1)
        return 0

    assert n_gu == n_t
    lax.fori_loop(0, n_t, fused, 0)
    for b in range(nb):
        gather_sends_done(L1, b)

    def z_loop1(t, _):
        wslot = lax.rem(t, 2)
        wait_out(wslot)

        @pl.when(t + 1 < n_t)
        def _():
            load_out(L1, t + 1, 1 - wslot)
        j = j_end + n_t + t
        z_step(1, wslot, j)
        rs_b(j - 1)
        i2 = n_t + t - 2
        rs_c(L1, j - 2, lax.div(i2, n_t), lax.rem(i2, n_t))
        return 0

    lax.fori_loop(0, n_t, z_loop1, 0)
    j_last = 2 * j_end - 1
    rs_b(j_last)
    rs_c(L1, j_last - 1, 1, n_t - 2)
    rs_c(L1, j_last, 1, n_t - 1)
    for b in range(nb):
        combine(L1, b)
    yout = pltpu.make_async_copy(xv, y_ref, misc.at[0])
    yout.start()
    layer_sends_done(L0)
    layer_sends_done(L1)
    for i in range(3):
        rc(gain_ref, gsl(d), g_s.at[i], g_r.at[i], g_to[i]).wait_send()

    @pl.when(c == 1)
    def _():
        for l in range(nl):
            rc(kl_ref, klb.at[l], k_s.at[l], k_r.at[l], other).wait_send()
    for slot in range(NS):
        c_wait(L1, slot)
        for way in range(2):
            a_send(slot, way).wait_send()
            b_send(slot, way).wait_send()
    yout.wait()


def solution(mesh):
    n_data = mesh.shape['data']
    n_x = mesh.shape['model'] // 2
    batch_axes = ('rep', 'data')

    def device_step(x_loc, len_loc, gain_loc, w_in_loc, w_attn_loc, w_mlp_loc):
        nl, dloc, block_in = w_in_loc.shape
        qw, ff = w_attn_loc.shape[1], w_mlp_loc.shape[1]
        hd = (block_in - qw - 2 * ff) // 2
        nb, sl, dm = x_loc.shape
        seq = sl * 2 * n_x
        cfg = (n_data, n_x, nb, sl, dm, dloc, qw, hd, ff, nl)
        cw = 512
        n_u = 2 + ff // (cw // 2) + dloc // cw
        n_t = n_data * (dloc // cw)
        lens = jnp.broadcast_to(len_loc[:, None, None], (nb, 8, 128))
        gain = jnp.broadcast_to(gain_loc.astype(F32)[:, None, :], (nl, 8, dloc))
        anyspec = pl.BlockSpec(memory_space=pl.ANY)
        vspec = pl.BlockSpec(memory_space=pltpu.VMEM)
        sem = pltpu.SemaphoreType.DMA
        out = pl.pallas_call(
            functools.partial(kernel, cfg),
            out_shape=[
                jax.ShapeDtypeStruct((nb, sl, dm), BF),
                jax.ShapeDtypeStruct((nl, n_data, dloc, block_in), BF),
                jax.ShapeDtypeStruct((nl, n_data, qw, dloc), BF),
                jax.ShapeDtypeStruct((nl, n_data, ff, dloc), BF),
            ],
            in_specs=[anyspec, vspec, vspec, anyspec, anyspec, anyspec],
            out_specs=[anyspec] * 4,
            scratch_shapes=[
                pltpu.VMEM((nb, seq, dm), BF),
                pltpu.VMEM((nb, seq, qw + 2 * hd), BF),
                pltpu.VMEM((nb, seq, qw + ff), BF),
                pltpu.VMEM((2, dm, cw), BF),
                pltpu.VMEM((NS, seq, cw), BF),
                pltpu.VMEM((NS, 2, 2 * sl, cw // 2), BF),
                pltpu.VMEM((NS, 2, 2 * sl, cw), BF),
                pltpu.VMEM((NS, 2 * sl, cw), BF),
                pltpu.VMEM((2, nb, sl, dm), BF),
                pltpu.VMEM((nb, sl, dm), BF),
                pltpu.VMEM((nb, sl, dm), BF),
                pltpu.VMEM((nl, 8, dm), F32),
                pltpu.VMEM((nl, nb, 8, 128), jnp.int32),
                pltpu.VMEM((nb, 8, 128), jnp.int32),
            ] + [sem((nl * n_u * 2,))] * 8 + [
                sem((2,)),
                sem((1,)),
                sem((3,)), sem((3,)),
                sem((nl,)), sem((nl,)),
                sem((nl * nb,)), sem((nl * nb * 2,)),
                sem((nl * nb,)), sem((nl * nb,)),
                sem((nl * nb * 2,)), sem((nl * nb * 2,)),
                sem((nl * nb * 2,)), sem((nl * nb * 2,)),
                sem((NS * 2,)), sem((NS * 2,)), sem((NS * 2,)), sem((NS * 2,)), sem((NS * 2,)),
                sem((nl * n_t * nb,)), sem((nl * n_t * nb,)),
                pltpu.SemaphoreType.REGULAR,
            ],
            compiler_params=pltpu.CompilerParams(collective_id=0, has_side_effects=True, vmem_limit_bytes=63 * 1024 * 1024),
        )(x_loc, lens, gain, w_in_loc, w_attn_loc, w_mlp_loc)
        return out[0]

    return jax.shard_map(device_step, mesh=mesh, in_specs=(P(batch_axes, 'model', None), P(batch_axes), P(None, 'data'), P(None, 'data', 'model'), P(None, 'model', 'data'), P(None, 'model', 'data')), out_specs=P(batch_axes, 'model', None), check_vma=False)
```

time: 1600 us -> 866 us (0.54)
  waiting for transfers between devices: 1090 us -> 0 us
  Pallas kernels: 0 us -> 853 us
  matrix products: 398 us -> 0 us
  other arithmetic: 48.3 us -> 0 us
  blocking collectives: 20.6 us -> 0 us
  local copies, waits for them, and re-layouts: 24.6 us -> 5.77 us
    all_gather x8 -> x0, waiting for transfers between devices: 917 us -> none  [the longest x2 684 us: device_step(): w_in_full = lax.all_gather(w_in_loc[layer_idx], 'data', axis=0, tiled=True)]
    pallas_call x0 -> x1, Pallas kernels: none -> 853 us  [device_step(): pl.pallas_call(functools.partial(kernel, cfg), out_shape=[jax.ShapeDtypeS...]
    dot_general x10 -> x0, matrix products: 398 us -> none  [the longest x2 192 us: device_step(): jnp.dot(h_full, w_in_full, preferred_element_type=jnp.float32)]
    reduce_scatter x2 -> x0, waiting for transfers between devices: 171 us -> none  [device_step(): lax.psum_scatter(group_part, 'model', scatter_dimension=1, tiled=True)]
    reduce_sum x6 -> x0, other arithmetic: 36.1 us -> none  [the longest x2 28.7 us: device_step(): soft_probs = jax.nn.softmax(scores, axis=-1)]
    slice x4 -> x0, local copies, waits for them, and re-layouts: 24 us -> none  [the longest x1 14.9 us: device_step(): w_in_full = lax.all_gather(w_in_loc[layer_idx], 'data', axis=0, tiled=True)]
    all_gather x2 -> x0, blocking collectives: 20.6 us -> none  [device_step(): gain_full = lax.all_gather(gain_loc[layer_idx], 'data', axis=0, tiled=True)]
  transfers between devices with their start and end apart: 10 -> 0, of which waited for: 8 -> 0; matrix products, arithmetic and copies ran while one was open for 26% -> 0% of each run, Pallas kernels for 0% -> 0%
where the time goes in v1:
time: 866 us; the launch traced here: 859 us
  Pallas kernels  853 us (98%)
    pallas_call x1, Pallas kernels, device_step(): pl.pallas_call(functools.partial(kernel, cfg), out_shape=[jax.ShapeDtypeS...  853 us

profile of v1, /device:TPU:97, one launch (start us, length us, event | category | flops | bytes accessed | tf_op | source)
XLA Modules:
  0.0 859.0 jit_solution(8355721583027415548)
XLA Ops:
  0.0 1.3 broadcast_in_dim.4.kl_ref
  1.3 1.3 broadcast_in_dim.5.gain_ref
  2.6 852.8 %shard_map.64 = (bf16[2,128,4096]{2,1,0:T(8,128)(2,1)}, bf16[2,4,1024,4864]{3,2,1,0:T(8,128)(2,1)}, bf16[2,4,512,1024]{3,2,1,0:T(8,128)(2,1)}, bf16[2,4,2048,1024]{3,2,1,0:T(8,128)(2,1)}) custom-call(bf16[2,128,4096]{2,1,0:T(8,128)(2,1)} %x_ref.1, s32[2,8,128]{2,1,0:T(8,128)} %broadcast_in_dim.4.kl_ref, f32[2,8,1024]{2,1,0:T(8,128)} %broadcast_in_dim.5.gain_ref, ...), custom_call_target="tpu_custom_call" | custom-call | tf_op jit(solution)/shard_map/pallas_call | solution.py:788
  855.4 3.1 copy.8

commit v2 on v1

v2 whole, which is shorter than its diff:
```python
import functools

import jax
import jax.numpy as jnp
from jax import lax
from jax.experimental import pallas as pl
from jax.experimental.pallas import tpu as pltpu
from jax.sharding import PartitionSpec as P

EPSILON = 1e-6
NEG_BIG = -1e30
MESH = pl.DeviceIdType.MESH
BF = jnp.bfloat16
F32 = jnp.float32
NS = 3
NC = 4


def kernel(cfg, x_ref, kl_ref, gain_ref, wi_ref, wa_ref, wm_ref,
           y_ref, wi_buf, wa_buf, wm_buf,
           hv, qkv, om, wv, wz, zs, ra, rb, cst, parts, xv, hs, gfull, klb, kcur,
           w_r1, w_r2, w_d1, w_d2, w_s1, w_s2, w_s3, w_s4, wld, wzs, misc,
           g_s, g_r, k_s, k_r, ax_s, ax_r, ad_s, ad_r, rg_s, rg_r, rf_s, rf_r,
           a_s, a_r, b_s, b_r, c_s, pd_r, pa_r, free_sem):
    (n_data, n_x, nb, sl, dm, dloc, qw, hd, ff, nl) = cfg
    seq = sl * 2 * n_x
    blk = 2 * sl
    cw = 512
    hw = cw // 2
    kv0 = qw
    ff0 = qw + 2 * hd
    n_gu = ff // hw
    n_in = 2 + n_gu
    n_out = dloc // cw
    n_u = n_in + n_out
    n_t = n_data * n_out
    rw = qw + ff

    d = lax.axis_index('data')
    m = lax.axis_index('model')
    x = lax.div(m, 2)
    c = lax.rem(m, 2)
    d_odd = lax.rem(d, 2)
    nbr1 = d + 1 - 2 * d_odd
    nbr3 = n_data - 1 - d
    opp = lax.rem(d + 2, n_data)
    xr = lax.rem(x + 1, n_x)
    xl = lax.rem(x + n_x - 1, n_x)
    xo = lax.rem(x + 2, n_x)

    home, away = c == 0, c == 1

    def dev(dd, xx, cc):
        return {'data': dd, 'model': xx * 2 + cc}

    def rc(src, dst, ss, rs, to):
        return pltpu.make_async_remote_copy(src_ref=src, dst_ref=dst, send_sem=ss, recv_sem=rs, device_id=to, device_id_type=MESH)

    other = dev(d, x, 1 - c)
    right = dev(d, xr, c)
    left = dev(d, xl, c)

    class Lay:
        pass

    lays = []
    for l in range(nl):
        L = Lay()
        L.l = l
        if l % 2 == 0:
            L.p, L.q, a = nbr1, nbr3, lax.div(d, 2)
        else:
            L.p, L.q, a = nbr3, nbr1, lax.rem(lax.div(d + 1, 2), 2)
        L.isb = (c - a) * (c - a)
        L.a_core, L.b_core = L.isb == 0, L.isb == 1
        L.src1 = L.p + (L.q - L.p) * L.isb
        L.srcx = L.q + (L.p - L.q) * L.isb
        L.src2 = opp + (d - opp) * L.isb
        L.first = dev(L.src1, x, c + (1 - 2 * c) * L.isb)
        L.pair = dev(L.p, x, c)
        lays.append(L)

    barrier = pltpu.get_barrier_semaphore()
    friends = [other, right, left, dev(nbr1, x, 0), dev(nbr1, x, 1), dev(nbr3, x, 0), dev(nbr3, x, 1), dev(opp, x, c)]
    for f in friends:
        pl.semaphore_signal(barrier, inc=1, device_id=f, device_id_type=MESH)
    xload = pltpu.make_async_copy(x_ref, xv, misc.at[0])
    xload.start()
    pl.semaphore_wait(barrier, len(friends))

    def cols(start, width):
        return pl.ds(start if isinstance(start, int) else pl.multiple_of(start, 128), width)

    class Unit:
        def __init__(self, L, s, parts_):
            self.L, self.idx, self.parts = L, (L.l * n_u + s) * 2, parts_

    def unit_in(L, s):
        l = L.l
        nz = min(s, 1) if isinstance(s, int) else lax.div(s + n_u - 1, n_u)
        starts = [hw + hw * s, (ff0 + ff + hw * (s - 2)) * nz]

        def part(c0):
            return (wi_ref.at[l, :, cols(c0, hw)], lambda e: wi_buf.at[l, e, :, cols(c0, hw)])
        u = Unit(L, s, [part(c0) for c0 in starts])
        u.s = s
        return u

    def each(u, fn):
        for i, (own, buf) in enumerate(u.parts):
            s = getattr(u, 's', 0)
            if i == 0 or (isinstance(s, int) and s != 1):
                fn(i, own, buf)
            elif not isinstance(s, int):
                @pl.when(s != 1)
                def _():
                    fn(i, own, buf)

    def unit_out(L, v):
        l = L.l
        cc = cols(v * cw, cw)
        return Unit(L, n_in + v, [(wa_ref.at[l, :, cc], lambda e: wa_buf.at[l, e, :, cc]), (wm_ref.at[l, :, cc], lambda e: wm_buf.at[l, e, :, cc])])

    def send_own(u, cond=None):
        L = u.L

        def go(i, own, buf):
            rc(own, buf(d), w_s1.at[u.idx + i], w_r1.at[u.idx + i], L.first).start()

        def go2(i, own, buf):
            rc(own, buf(d), w_s3.at[u.idx + i], w_d2.at[u.idx + i], other).start()

        if cond is None:
            each(u, go)
        else:
            @pl.when(L.a_core if cond == 'a' else L.b_core)
            def _():
                each(u, go)
        if cond != 'b':
            @pl.when(L.a_core)
            def _():
                each(u, go2)

    def fwd1(u, cond=None):
        L = u.L

        def go(i, own, buf):
            rc(own, buf(L.src1), w_s1.at[u.idx + i], w_r1.at[u.idx + i], L.first).wait_recv()

            @pl.when(L.b_core)
            def _():
                rc(buf(L.src1), buf(L.src1), w_s4.at[u.idx + i], w_r2.at[u.idx + i], L.pair).start()
            rc(buf(L.src1), buf(L.src1), w_s2.at[u.idx + i], w_d1.at[u.idx + i], other).start()

        if cond is None:
            each(u, go)
        else:
            @pl.when(L.a_core if cond == 'a' else L.b_core)
            def _():
                each(u, go)

    def fwd2(u):
        L = u.L

        def go(i, own, buf):
            rc(own, buf(opp), w_s4.at[u.idx + i], w_r2.at[u.idx + i], L.pair).wait_recv()
            rc(buf(opp), buf(opp), w_s3.at[u.idx + i], w_d2.at[u.idx + i], other).start()

        @pl.when(L.b_core)
        def _():
            each(u, go)

    def got1(u):
        each(u, lambda i, own, buf: rc(own, buf(u.L.srcx), w_s2.at[u.idx + i], w_d1.at[u.idx + i], other).wait_recv())

    def got2(u):
        each(u, lambda i, own, buf: rc(own, buf(u.L.src2), w_s3.at[u.idx + i], w_d2.at[u.idx + i], other).wait_recv())

    def sends_done(u):
        L = u.L

        def go(i, own, buf):
            rc(own, buf(d), w_s1.at[u.idx + i], w_r1.at[u.idx + i], L.first).wait_send()
            rc(own, buf(d), w_s2.at[u.idx + i], w_d1.at[u.idx + i], other).wait_send()
            rc(own, buf(d), w_s3.at[u.idx + i], w_d2.at[u.idx + i], other).wait_send()

            @pl.when(L.b_core)
            def _():
                rc(own, buf(d), w_s4.at[u.idx + i], w_r2.at[u.idx + i], L.pair).wait_send()
        each(u, go)

    def load_in(u, slot):
        L = u.L

        def go(i, own, buf):
            def to(e):
                return wv.at[slot, pl.ds(pl.multiple_of(e * dloc, dloc), dloc), pl.ds(i * hw, hw)]

            for e in (L.p, L.q, opp):
                pltpu.make_async_copy(buf(e), to(e), wld.at[slot]).start()

            @pl.when(L.a_core)
            def _():
                pltpu.make_async_copy(own, to(d), wld.at[slot]).start()

            @pl.when(L.b_core)
            def _():
                pltpu.make_async_copy(buf(d), to(d), wld.at[slot]).start()
        each(u, go)

    def wait_in(slot, w):
        pltpu.make_async_copy(wv.at[slot, :, pl.ds(0, w)], wv.at[slot, :, pl.ds(0, w)], wld.at[slot]).wait()

    def z_src(L, t):
        n2 = 2 * n_out
        late, r = lax.div(t, n2), lax.rem(t, n2)
        if L.l == 0:
            k = (1 - late) * lax.div(r, n_out) + late * (2 + lax.rem(r, 2))
            v = (1 - late) * lax.rem(r, n_out) + late * lax.div(r, 2)
        else:
            k, v = late + 2 * lax.rem(lax.div(t, n_out), 2), lax.rem(t, n_out)
        src = jnp.where(k == 0, d, jnp.where(k == 1, L.q, jnp.where(k == 2, L.p, opp)))
        return k, v, src

    def z_col(L, t):
        _, v, src = z_src(L, t)
        return src * n_out + v

    def load_out(L, t, wref, wsem):
        k, v, src = z_src(L, t)
        u = unit_out(L, v)
        spots = (wref.at[pl.ds(0, qw), :], wref.at[pl.ds(qw, ff), :])
        mine = jnp.logical_and(k == 0, L.a_core)

        @pl.when(mine)
        def _():
            for (own, buf), to in zip(u.parts, spots):
                pltpu.make_async_copy(own, to, wsem).start()

        @pl.when(jnp.logical_not(mine))
        def _():
            for (own, buf), to in zip(u.parts, spots):
                pltpu.make_async_copy(buf(src), to, wsem).start()

    def wait_out(wref, wsem):
        ref = wref.at[pl.ds(0, rw), :]
        pltpu.make_async_copy(ref, ref, wsem).wait()

    def wslot_of(slot):
        return wv.at[slot], wld.at[slot]

    def out_arrives(L, t):
        k, v, src = z_src(L, t)
        u = unit_out(L, v)

        @pl.when(jnp.logical_and(k == 0, L.b_core))
        def _():
            got2(u)

        @pl.when(jnp.logical_and(k == 1, L.a_core))
        def _():
            got1(u)

        if L.l == 0:
            @pl.when(jnp.logical_and(k == 2, L.a_core))
            def _():
                fwd1(u)

        @pl.when(jnp.logical_and(k == 2, L.b_core))
        def _():
            got1(u)

        if L.l == 0:
            @pl.when(k == 3)
            def _():
                fwd2(u)

        @pl.when(jnp.logical_and(k == 3, L.a_core))
        def _():
            got2(u)

    rows = 32

    def layer_norm(L, b):
        g = gfull[L.l:L.l + 1, :]

        def tile(i, _):
            r = pl.ds(pl.multiple_of(i * rows, rows), rows)
            v = xv[b, r, :].astype(F32)
            cen = v - jnp.mean(v, axis=-1, keepdims=True)
            var = jnp.mean(cen * cen, axis=-1, keepdims=True)
            h = (cen * lax.rsqrt(var + EPSILON) * g).astype(BF)
            hs[b, r, :] = h

            @pl.when(home)
            def _():
                hv[b, pl.ds(pl.multiple_of(m * sl + i * rows, rows), rows), :] = h
            return 0

        lax.fori_loop(0, sl // rows, tile, 0)

    def my_rows(b):
        return hv.at[b, pl.ds(pl.multiple_of(m * sl, sl), sl), :]

    def block(b, xx, lo=0, n=None):
        return hv.at[b, pl.ds(pl.multiple_of(xx * blk, blk), blk), pl.ds(lo, dm if n is None else n)]

    def ax(L, b):
        i = L.l * nb + b
        return rc(hs.at[b], my_rows(b), ax_s.at[i], ax_r.at[2 * i + c], dev(L.q, x, 1))

    def ad(L, b):
        i = L.l * nb + b
        return rc(hs.at[b], my_rows(b), ad_s.at[i], ad_r.at[i], other)

    def share(L, b):
        ax(L, b).start()

        @pl.when(away)
        def _():
            ad(L, b).start()

    def ring(L, b, way):
        i = 2 * (L.l * nb + b) + way
        return rc(block(b, x), block(b, x), rg_s.at[i], rg_r.at[i], right if way == 0 else left)

    def ring_in(L, b, way):
        i = 2 * (L.l * nb + b) + way
        src = block(b, xl if way == 0 else xr)
        return rc(src, src, rg_s.at[i], rg_r.at[i], right if way == 0 else left)

    def ring2(L, b, way, xx):
        i = 2 * (L.l * nb + b) + way
        src = block(b, xx, 0 if way == 0 else dm // 2, dm // 2)
        return rc(src, src, rf_s.at[i], rf_r.at[i], right if way == 0 else left)

    def ring_start(L, b):
        i = L.l * nb + b

        @pl.when(home)
        def _():
            dst = hv.at[b, pl.ds(pl.multiple_of(x * blk + sl, sl), sl), :]
            rc(hs.at[b], dst, ad_s.at[i], ad_r.at[i], other).wait_recv()

        @pl.when(away)
        def _():
            for cc in range(2):
                dst = hv.at[b, pl.ds(pl.multiple_of(x * blk + cc * sl, sl), sl), :]
                rc(hs.at[b], dst, ax_s.at[i], ax_r.at[2 * i + cc], other).wait_recv()
        for way in range(2):
            ring(L, b, way).start()

    def ring_pass(L, b):
        for way in range(2):
            ring_in(L, b, way).wait_recv()
            ring2(L, b, way, xl if way == 0 else xr).start()

    def ring_end(L, b):
        for way in range(2):
            ring2(L, b, way, xo).wait_recv()

    def gather_sends_done(L, b):
        ax(L, b).wait_send()

        @pl.when(away)
        def _():
            ad(L, b).wait_send()
        for way in range(2):
            ring(L, b, way).wait_send()
            ring2(L, b, way, xl if way == 0 else xr).wait_send()

    def p_qkv(b):
        def step(i, _):
            col = hw * (1 - i) + 3 * hw * lax.div(i, 2)
            w = wv[lax.div(i, 2), :, cols(lax.rem(i, 2) * hw, hw)]
            qkv[b, :, cols(col, hw)] = jnp.dot(hv[b], w, preferred_element_type=F32).astype(BF)
            return 0
        lax.fori_loop(0, 3, step, 0)

    def p_gu(b, slot, k):
        acc = jnp.dot(hv[b], wv[slot], preferred_element_type=F32)
        g = acc[:, 0:hw].astype(BF).astype(F32)
        up = acc[:, hw:cw].astype(BF).astype(F32)
        om[b, :, cols(qw + hw * k, hw)] = (g * (1.0 / (1.0 + jnp.exp(-g))) * up).astype(BF)

    def attention(b):
        tq = 256
        kl = kcur[b, 0:1, 0:1]
        for i in range(seq // tq):
            n = tq * (i + 1)
            row = lax.broadcasted_iota(jnp.int32, (tq, n), 0) + tq * i
            col = lax.broadcasted_iota(jnp.int32, (tq, n), 1)
            ok = jnp.logical_and(col <= row, col < kl)

            def head(h, _):
                hc = pl.ds(pl.multiple_of(h * hd, hd), hd)
                qh = qkv[b, tq * i:tq * (i + 1), hc]
                s = lax.dot_general(qh, qkv[b, 0:n, kv0:kv0 + hd], (((1,), (1,)), ((), ())), preferred_element_type=F32) * hd ** -0.5
                s = jnp.where(ok, s, NEG_BIG)
                e = jnp.exp(s - jnp.max(s, axis=-1, keepdims=True))
                tot = jnp.sum(e, axis=-1, keepdims=True)
                o = jnp.dot(e.astype(BF), qkv[b, 0:n, kv0 + hd:kv0 + 2 * hd], preferred_element_type=F32)
                om[b, tq * i:tq * (i + 1), hc] = (o / tot).astype(BF)
                return 0

            lax.fori_loop(0, qw // hd, head, 0)

    def zblk(slot, xx, lo, n):
        return zs.at[slot, pl.ds(pl.multiple_of(xx * blk, blk), blk), pl.ds(lo, n)]

    def a_send(slot, way):
        return rc(zblk(slot, xo, way * hw, hw), ra.at[slot, way], a_s.at[2 * slot + way], a_r.at[2 * slot + way], right if way == 0 else left)

    def b_send(slot, way):
        return rc(zblk(slot, xr if way == 0 else xl, 0, cw), rb.at[slot, way], b_s.at[2 * slot + way], b_r.at[2 * slot + way],
                  right if way == 0 else left)

    def z_step(b, wref, j):
        slot = lax.rem(j, NS)

        @pl.when(j >= NS)
        def _():
            for way in range(2):
                a_send(slot, way).wait_send()
                b_send(slot, way).wait_send()
        zs[slot] = jnp.dot(om[b], wref[0:rw, :], preferred_element_type=F32).astype(BF)
        for way in range(2):
            a_send(slot, way).start()

    def rs_b(j):
        slot = lax.rem(j, NS)
        for way in range(2):
            a_send(slot, way).wait_recv()
            r = pl.ds(pl.multiple_of((xr if way == 0 else xl) * blk, blk), blk)
            cc = pl.ds(way * hw, hw)
            zs[slot, r, cc] = (zs[slot, r, cc].astype(F32) + ra[slot, way].astype(F32)).astype(BF)
        for way in range(2):
            b_send(slot, way).start()

    def c_send(L, b, n, slot, cc, inside):
        i = (L.l * n_t + n) * nb + b
        sem = c_s.at[2 * slot + cc]
        if inside:
            return rc(cst.at[slot, pl.ds(cc * sl, sl), :], parts.at[0, b, :, cols(n * cw, cw)], sem, pd_r.at[i], other)
        return rc(cst.at[slot, pl.ds(cc * sl, sl), :], parts.at[1, b, :, cols(n * cw, cw)], sem, pa_r.at[i], dev(L.q, x, cc))

    def c_wait(L, slot):
        @pl.when(away)
        def _():
            for cc in range(2):
                c_send(L, 0, 0, slot, cc, False).wait_send()

        @pl.when(home)
        def _():
            c_send(L, 0, 0, slot, 1, True).wait_send()

    def rs_c(L, j, b, t):
        slot, cslot = lax.rem(j, NS), lax.rem(j, NC)
        n = z_col(L, t)
        for way in range(2):
            b_send(slot, way).wait_recv()

        @pl.when(j >= NC)
        def _():
            c_wait(L, cslot)
        r = pl.ds(pl.multiple_of(x * blk, blk), blk)
        cst[cslot] = (zs[slot, r, :].astype(F32) + rb[slot, 0].astype(F32) + rb[slot, 1].astype(F32)).astype(BF)

        @pl.when(home)
        def _():
            c_send(L, b, n, cslot, 1, True).start()
            parts[0, b, :, cols(n * cw, cw)] = cst[cslot, 0:sl, :]

        @pl.when(away)
        def _():
            for cc in range(2):
                c_send(L, b, n, cslot, cc, False).start()

    def combine(L, b):
        for n in range(n_t):
            c_send(L, b, n, 0, 0, False).wait_recv()

            @pl.when(away)
            def _():
                c_send(L, b, n, 0, 0, True).wait_recv()

        def tile(i, _):
            r = pl.ds(pl.multiple_of(i * rows, rows), rows)
            z = parts[0, b, r, :].astype(F32) + parts[1, b, r, :].astype(F32)
            xv[b, r, :] = (xv[b, r, :].astype(F32) + z).astype(BF)
            return 0

        lax.fori_loop(0, sl // rows, tile, 0)

    L0, L1 = lays
    g_to = [dev(nbr1, x, c), dev(nbr3, x, c), dev(opp, x, c)]

    def gsl(e):
        return gfull.at[:, pl.ds(pl.multiple_of(e * dloc, dloc), dloc)]

    for i in range(3):
        rc(gain_ref, gsl(d), g_s.at[i], g_r.at[i], g_to[i]).start()

    @pl.when(away)
    def _():
        for l, L in enumerate(lays):
            rc(kl_ref, klb.at[l], k_s.at[l], k_r.at[l], dev(L.q, x, 1)).start()
    gfull[:, pl.ds(pl.multiple_of(d * dloc, dloc), dloc)] = gain_ref[...]

    def set_len(L):
        @pl.when(home)
        def _():
            kcur[...] = kl_ref[...]

        @pl.when(away)
        def _():
            rc(kl_ref, klb.at[L.l], k_s.at[L.l], k_r.at[L.l], other).wait_recv()
            kcur[...] = klb[L.l]

    def loop(n, fn, start=0):
        def body(i, _):
            fn(i)
            return 0
        lax.fori_loop(start, n, body, 0)

    def both(*conds):
        r = conds[0]
        for q in conds[1:]:
            r = jnp.logical_and(r, q)
        return r

    xload.wait()
    for i, e in enumerate((nbr1, nbr3, opp)):
        rc(gain_ref, gsl(e), g_s.at[i], g_r.at[i], g_to[i]).wait_recv()
    loop(n_in, lambda s: send_own(unit_in(L0, s), 'a'))
    layer_norm(L0, 0)
    share(L0, 0)
    layer_norm(L0, 1)
    loop(2, lambda s: send_own(unit_in(L0, s), 'b'))
    share(L0, 1)
    loop(n_in, lambda s: send_own(unit_in(L0, s), 'b'), 2)
    loop(n_out, lambda v: send_own(unit_out(L0, v), 'b'))
    set_len(L0)

    def in_ready(L, s):
        u = unit_in(L, s)
        fwd2(u)
        got1(u)
        got2(u)

    def fa(L, s):
        fwd1(unit_in(L, s), 'a')

    def fb(L, s):
        fwd1(unit_in(L, s), 'b')

    ring_start(L0, 0)
    for s in range(3):
        fa(L0, s)

    @pl.when(home)
    def _():
        ring_pass(L0, 0)
    fb(L0, 0)
    fb(L0, 1)
    fa(L0, 3)

    @pl.when(away)
    def _():
        ring_pass(L0, 0)
    fa(L0, 4)
    ring_start(L0, 1)
    fwd2(unit_in(L0, 0))
    fa(L0, 5)
    fb(L0, 2)
    fwd2(unit_in(L0, 1))
    ring_end(L0, 0)
    n_early = 2

    def stage0(b):
        first = b == 0

        @pl.when(first)
        def _():
            for s in range(2):
                got1(unit_in(L0, s))
                got2(unit_in(L0, s))

        @pl.when(jnp.logical_not(first))
        def _():
            fb(L0, 7)
            ring_end(L0, 1)
        load_in(unit_in(L0, 0), 0)
        load_in(unit_in(L0, 1), 1)
        wait_in(0, cw)
        wait_in(1, hw)
        p_qkv(b)

        @pl.when(first)
        def _():
            fb(L0, 3)
        attention(b)

        @pl.when(first)
        def _():
            fb(L0, 4)
            fa(L0, 6)
            in_ready(L0, 2)

        @pl.when(jnp.logical_not(first))
        def _():
            fb(L0, 8)
            fa(L0, 8)
        load_in(unit_in(L0, 2), 0)

        def gu(k):
            slot = lax.rem(k, 2)
            wait_in(slot, cw)
            p_gu(b, slot, k)

            @pl.when(both(first, k == 0))
            def _():
                fb(L0, 5)
                ring_pass(L0, 1)
                fb(L0, 6)
                fa(L0, 7)
                in_ready(L0, 3)

            @pl.when(both(jnp.logical_not(first), k == 0))
            def _():
                fwd2(unit_in(L0, 4))

            @pl.when(k + 1 < n_early)
            def _():
                load_in(unit_in(L0, k + 3), 1 - slot)
        loop(n_early, gu)

    loop(nb, stage0)
    fb(L0, 9)
    u4 = unit_in(L0, n_early + 2)
    got1(u4)
    got2(u4)
    load_in(u4, n_early % 2)

    def gu0(k):
        s = k + 2
        slot = lax.rem(k, 2)
        wait_in(slot, cw)
        p_gu(0, slot, k)

        @pl.when(k == n_early)
        def _():
            fa(L0, 9)

        @pl.when(both(k >= n_gu - 1 - n_out, k < n_gu - 1))
        def _():
            fwd1(unit_out(L0, k - (n_gu - 1 - n_out)), 'b')

        @pl.when(k == n_gu // 2)
        def _():
            loop(n_out, lambda v: send_own(unit_out(L0, v), 'a'))

        @pl.when(s + 1 < n_in)
        def _():
            in_ready(L0, s + 1)
            load_in(unit_in(L0, s + 1), 1 - slot)

        @pl.when(s + 1 == n_in)
        def _():
            out_arrives(L0, 0)
            load_out(L0, 0, *wslot_of(1 - slot))
        p_gu(1, slot, k)

        @pl.when(both(k >= n_gu - 4, k < n_gu - 2))
        def _():
            for i in range(2):
                send_own(unit_in(L1, 2 * (k - (n_gu - 4)) + i), 'a')

        @pl.when(k >= n_gu - 2)
        def _():
            send_own(unit_in(L1, k - (n_gu - 2) + 4), 'a')

    loop(n_gu, gu0, n_early)
    for b in range(nb):
        gather_sends_done(L0, b)

    @pl.when(away)
    def _():
        for cc in range(2):
            pl.semaphore_signal(free_sem, inc=1, device_id=dev(L1.q, x, cc), device_id_type=MESH)
    z0 = n_gu % 2
    j_end = nb * n_t
    j_late = j_end // 2

    assert nb == 2 and n_t == 8

    def pick(i, values):
        r = values[-1]
        for k in range(len(values) - 1):
            r = jnp.where(i == k, values[k], r)
        return r

    def jt(j):
        late, r = lax.div(j, j_late), lax.rem(j, j_late)
        b = (1 - late) * lax.rem(r, nb) + late * pick(r, (0, 0, 1, 0, 0, 1, 1, 1))
        t = (1 - late) * lax.div(r, nb) + late * (n_t // 2 + pick(r, (0, 1, 0, 2, 3, 1, 2, 3)))
        return b, t

    def z_loop0(j):
        slot = lax.rem(j + z0, 2)
        b, t = jt(j)
        wait_out(*wslot_of(slot))
        z_step(b, wv.at[slot], j)

        @pl.when(j + 1 < j_end)
        def _():
            b1, t1 = jt(j + 1)

            @pl.when(b1 == 0)
            def _():
                out_arrives(L0, t1)
            load_out(L0, t1, *wslot_of(1 - slot))

        @pl.when(j >= 1)
        def _():
            rs_b(j - 1)

        @pl.when(j >= 2)
        def _():
            b2, t2 = jt(j - 2)
            rs_c(L0, j - 2, b2, t2)
        half = lax.div(j, 2)

        @pl.when(both(lax.rem(j, 2) == 1, half + 6 < n_in))
        def _():
            send_own(unit_in(L1, half + 6), 'a')

        @pl.when(lax.rem(j, 2) == 1)
        def _():
            fa(L1, half)

        @pl.when(j == j_late)
        def _():
            send_own(unit_out(L1, 0), 'a')

        @pl.when(both(j >= j_end - 5, lax.rem(j, 2) == 1, j < j_end - 1))
        def _():
            for i in range(2):
                send_own(unit_in(L1, j - (j_end - 5) + i), 'b')

    loop(j_end, z_loop0)
    pl.semaphore_wait(free_sem, 1)
    combine(L0, 0)
    layer_norm(L1, 0)
    share(L1, 0)
    rs_b(j_end - 1)
    rs_c(L0, j_end - 2, nb - 1, n_t - 2)
    rs_c(L0, j_end - 1, nb - 1, n_t - 1)

    @pl.when(home)
    def _():
        ring_start(L1, 0)
    for s in range(3):
        fb(L1, s)
    combine(L0, 1)
    layer_norm(L1, 1)
    share(L1, 1)
    send_own(unit_in(L1, 4), 'b')
    loop(n_in, lambda s: send_own(unit_in(L1, s), 'b'), 5)
    loop(n_out, lambda v: send_own(unit_out(L1, v), 'b'))
    loop(n_in, lambda s: fa(L1, s), n_in - 2)
    set_len(L1)

    @pl.when(away)
    def _():
        ring_start(L1, 0)
    fb(L1, 3)
    in_ready(L1, 0)
    load_in(unit_in(L1, 0), 0)
    in_ready(L1, 1)
    load_in(unit_in(L1, 1), 1)

    @pl.when(home)
    def _():
        ring_pass(L1, 0)
    fwd2(unit_in(L1, 2))
    send_own(unit_out(L1, 1), 'a')
    fb(L1, 4)

    @pl.when(away)
    def _():
        ring_pass(L1, 0)
        ring_start(L1, 1)
    fb(L1, 5)
    fwd2(unit_in(L1, 3))
    fb(L1, 6)
    fwd2(unit_in(L1, 4))
    assert n_gu == n_t

    def stage1(b):
        first = b == 0

        @pl.when(jnp.logical_not(first))
        def _():
            load_in(unit_in(L1, 0), 0)
            load_in(unit_in(L1, 1), 1)
        ring_end(L1, b)
        wait_in(0, cw)
        wait_in(1, hw)
        p_qkv(b)

        @pl.when(first)
        def _():
            fb(L1, 7)
            fwd2(unit_in(L1, 5))
            got1(unit_in(L1, 2))
            got2(unit_in(L1, 2))

        @pl.when(both(first, home))
        def _():
            ring_start(L1, 1)
        load_in(unit_in(L1, 2), 0)

        @pl.when(jnp.logical_not(first))
        def _():
            fwd1(unit_out(L1, 1), 'b')
            out_arrives(L1, 0)
            load_out(L1, 0, wz, wzs.at[0])
        attention(b)

        @pl.when(first)
        def _():
            fb(L1, 8)
            fwd2(unit_in(L1, 6))

        def gu(k):
            slot = lax.rem(k, 2)

            @pl.when(both(first, k == 0))
            def _():
                fb(L1, n_in - 1)

            @pl.when(both(first, k + 7 < n_in))
            def _():
                fwd2(unit_in(L1, k + 7))

            @pl.when(both(first, k >= n_gu - n_out))
            def _():
                fwd1(unit_out(L1, k - (n_gu - n_out)), 'a')

            @pl.when(both(first, k == n_gu - 2))
            def _():
                fwd1(unit_out(L1, 0), 'b')

            @pl.when(both(jnp.logical_not(first), k >= 3, k < 3 + n_out))
            def _():
                fwd2(unit_out(L1, k - 3))

            @pl.when(both(first, k + 1 < n_gu))
            def _():
                got1(unit_in(L1, k + 3))
                got2(unit_in(L1, k + 3))

            @pl.when(k + 1 < n_gu)
            def _():
                load_in(unit_in(L1, k + 3), 1 - slot)
            wait_in(slot, cw)
            p_gu(b, slot, k)

            @pl.when(both(first, k == 5))
            def _():
                ring_pass(L1, 1)

            @pl.when(jnp.logical_not(first))
            def _():
                wait_out(wz, wzs.at[0])
                j = j_end + k
                z_step(0, wz, j)

                @pl.when(k >= 1)
                def _():
                    rs_b(j - 1)

                @pl.when(k >= 2)
                def _():
                    rs_c(L1, j - 2, 0, k - 2)

                @pl.when(k + 1 < n_t)
                def _():
                    out_arrives(L1, k + 1)
                    load_out(L1, k + 1, wz, wzs.at[0])
        loop(n_gu, gu)

    loop(nb, stage1)
    load_out(L1, 0, *wslot_of(0))
    for b in range(nb):
        gather_sends_done(L1, b)

    def z_loop1(t):
        wslot = lax.rem(t, 2)
        wait_out(*wslot_of(wslot))

        @pl.when(t + 1 < n_t)
        def _():
            load_out(L1, t + 1, *wslot_of(1 - wslot))
        j = j_end + n_t + t
        z_step(1, wv.at[wslot], j)
        rs_b(j - 1)
        i2 = n_t + t - 2
        rs_c(L1, j - 2, lax.div(i2, n_t), lax.rem(i2, n_t))

    loop(n_t, z_loop1)
    j_last = 2 * j_end - 1
    rs_b(j_last)
    rs_c(L1, j_last - 1, 1, n_t - 2)
    rs_c(L1, j_last, 1, n_t - 1)
    for b in range(nb):
        combine(L1, b)
    yout = pltpu.make_async_copy(xv, y_ref, misc.at[0])
    yout.start()

    def layer_sends_done(L):
        loop(n_in, lambda s: sends_done(unit_in(L, s)))
        loop(n_out, lambda v: sends_done(unit_out(L, v)))

    layer_sends_done(L0)
    layer_sends_done(L1)
    for i in range(3):
        rc(gain_ref, gsl(d), g_s.at[i], g_r.at[i], g_to[i]).wait_send()

    @pl.when(away)
    def _():
        for l in range(nl):
            rc(kl_ref, klb.at[l], k_s.at[l], k_r.at[l], other).wait_send()
    for slot in range(NC):
        c_wait(L1, slot)
    for slot in range(NS):
        for way in range(2):
            a_send(slot, way).wait_send()
            b_send(slot, way).wait_send()
    yout.wait()


def solution(mesh):
    n_data = mesh.shape['data']
    n_x = mesh.shape['model'] // 2
    batch_axes = ('rep', 'data')

    def device_step(x_loc, len_loc, gain_loc, w_in_loc, w_attn_loc, w_mlp_loc):
        nl, dloc, block_in = w_in_loc.shape
        qw, ff = w_attn_loc.shape[1], w_mlp_loc.shape[1]
        hd = (block_in - qw - 2 * ff) // 2
        nb, sl, dm = x_loc.shape
        seq = sl * 2 * n_x
        cfg = (n_data, n_x, nb, sl, dm, dloc, qw, hd, ff, nl)
        cw = 512
        n_u = 2 + ff // (cw // 2) + dloc // cw
        n_t = n_data * (dloc // cw)
        lens = jnp.broadcast_to(len_loc[:, None, None], (nb, 8, 128))
        gain = gain_loc.astype(F32)
        anyspec = pl.BlockSpec(memory_space=pl.ANY)
        vspec = pl.BlockSpec(memory_space=pltpu.VMEM)
        sem = pltpu.SemaphoreType.DMA
        out = pl.pallas_call(
            functools.partial(kernel, cfg),
            out_shape=[
                jax.ShapeDtypeStruct((nb, sl, dm), BF),
                jax.ShapeDtypeStruct((nl, n_data, dloc, block_in), BF),
                jax.ShapeDtypeStruct((nl, n_data, qw, dloc), BF),
                jax.ShapeDtypeStruct((nl, n_data, ff, dloc), BF),
            ],
            in_specs=[anyspec, vspec, vspec, anyspec, anyspec, anyspec],
            out_specs=[anyspec] * 4,
            scratch_shapes=[
                pltpu.VMEM((nb, seq, dm), BF),
                pltpu.VMEM((nb, seq, qw + 2 * hd), BF),
                pltpu.VMEM((nb, seq, qw + ff), BF),
                pltpu.VMEM((2, dm, cw), BF),
                pltpu.VMEM((qw + ff, cw), BF),
                pltpu.VMEM((NS, seq, cw), BF),
                pltpu.VMEM((NS, 2, 2 * sl, cw // 2), BF),
                pltpu.VMEM((NS, 2, 2 * sl, cw), BF),
                pltpu.VMEM((NC, 2 * sl, cw), BF),
                pltpu.VMEM((2, nb, sl, dm), BF),
                pltpu.VMEM((nb, sl, dm), BF),
                pltpu.VMEM((nb, sl, dm), BF),
                pltpu.VMEM((nl, dm), F32),
                pltpu.VMEM((nl, nb, 8, 128), jnp.int32),
                pltpu.VMEM((nb, 8, 128), jnp.int32),
            ] + [sem((nl * n_u * 2,))] * 8 + [
                sem((2,)),
                sem((1,)),
                sem((1,)),
                sem((3,)), sem((3,)),
                sem((nl,)), sem((nl,)),
                sem((nl * nb,)), sem((nl * nb * 2,)),
                sem((nl * nb,)), sem((nl * nb,)),
                sem((nl * nb * 2,)), sem((nl * nb * 2,)),
                sem((nl * nb * 2,)), sem((nl * nb * 2,)),
                sem((NS * 2,)), sem((NS * 2,)), sem((NS * 2,)), sem((NS * 2,)), sem((NC * 2,)),
                sem((nl * n_t * nb,)), sem((nl * n_t * nb,)),
                pltpu.SemaphoreType.REGULAR,
            ],
            compiler_params=pltpu.CompilerParams(collective_id=0, has_side_effects=True, vmem_limit_bytes=63 * 1024 * 1024),
        )(x_loc, lens, gain, w_in_loc, w_attn_loc, w_mlp_loc)
        return out[0]

    return jax.shard_map(device_step, mesh=mesh, in_specs=(P(batch_axes, 'model', None), P(batch_axes), P(None, 'data'), P(None, 'data', 'model'), P(None, 'model', 'data'), P(None, 'model', 'data')), out_specs=P(batch_axes, 'model', None), check_vma=False)
```

time: 866 us -> 750 us (0.87)
  Pallas kernels: 853 us -> 736 us
    pallas_call x1, Pallas kernels: 853 us -> 736 us  [device_step(): pl.pallas_call(functools.partial(kernel, cfg), out_shape=[jax.ShapeDtypeS...]
where the time goes in v2:
time: 750 us; the launch traced here: 741 us
  Pallas kernels  736 us (98%)
    pallas_call x1, Pallas kernels, device_step(): pl.pallas_call(functools.partial(kernel, cfg), out_shape=[jax.ShapeDtypeS...  736 us

profile of v2, /device:TPU:97, one launch (start us, length us, event | category | flops | bytes accessed | tf_op | source)
XLA Modules:
  0.0 741.5 jit_solution(4943992061925035391)
XLA Ops:
  0.0 1.3 broadcast_in_dim.2.kl_ref
  1.3 1.3 convert_element_type.3.gain_ref
  2.6 735.8 %shard_map.64 = (bf16[2,128,4096]{2,1,0:T(8,128)(2,1)}, bf16[2,4,1024,4864]{3,2,1,0:T(8,128)(2,1)}, bf16[2,4,512,1024]{3,2,1,0:T(8,128)(2,1)}, bf16[2,4,2048,1024]{3,2,1,0:T(8,128)(2,1)}) custom-call(bf16[2,128,4096]{2,1,0:T(8,128)(2,1)} %x_ref.1, s32[2,8,128]{2,1,0:T(8,128)} %broadcast_in_dim.2.kl_ref, f32[2,1024]{1,0:T(2,128)} %convert_element_type.3.gain_ref, ...), custom_call_target="tpu_custom_call" | custom-call | tf_op jit(solution)/shard_map/pallas_call | solution.py:964
  738.4 3.1 copy.8

commit v3 on v2

--- a/solution.py
+++ b/solution.py
@@ -13,7 +13,7 @@
 BF = jnp.bfloat16
 F32 = jnp.float32
 NS = 3
-NC = 4
+NC = 8
 
 
 def kernel(cfg, x_ref, kl_ref, gain_ref, wi_ref, wa_ref, wm_ref,
@@ -743,10 +743,10 @@
         def _():
             send_own(unit_out(L1, 0), 'a')
 
-        @pl.when(both(j >= j_end - 5, lax.rem(j, 2) == 1, j < j_end - 1))
+        @pl.when(both(j >= j_end - 6, lax.rem(j, 2) == 0, j < j_end - 2))
         def _():
             for i in range(2):
-                send_own(unit_in(L1, j - (j_end - 5) + i), 'b')
+                send_own(unit_in(L1, j - (j_end - 6) + i), 'b')
 
     loop(j_end, z_loop0)
     pl.semaphore_wait(free_sem, 1)
@@ -797,6 +797,21 @@
     fwd2(unit_in(L1, 4))
     assert n_gu == n_t
 
+    n_lead = 2
+
+    def z_next(t):
+        @pl.when(t < n_t)
+        def _():
+            out_arrives(L1, t)
+            load_out(L1, t, wz, wzs.at[0])
+
+    def z_early(t):
+        wait_out(wz, wzs.at[0])
+        z_step(0, wz, j_end + t)
+        if t:
+            rs_b(j_end + t - 1)
+        z_next(t + 1)
+
     def stage1(b):
         first = b == 0
 
@@ -804,6 +819,8 @@
         def _():
             load_in(unit_in(L1, 0), 0)
             load_in(unit_in(L1, 1), 1)
+            fwd1(unit_out(L1, 1), 'b')
+            z_early(0)
         ring_end(L1, b)
         wait_in(0, cw)
         wait_in(1, hw)
@@ -823,9 +840,7 @@
 
         @pl.when(jnp.logical_not(first))
         def _():
-            fwd1(unit_out(L1, 1), 'b')
-            out_arrives(L1, 0)
-            load_out(L1, 0, wz, wzs.at[0])
+            z_early(1)
         attention(b)
 
         @pl.when(first)
@@ -852,9 +867,9 @@
             def _():
                 fwd1(unit_out(L1, 0), 'b')
 
-            @pl.when(both(jnp.logical_not(first), k >= 3, k < 3 + n_out))
-            def _():
-                fwd2(unit_out(L1, k - 3))
+            @pl.when(both(jnp.logical_not(first), k >= n_lead, k < n_lead + n_out))
+            def _():
+                fwd2(unit_out(L1, k - n_lead))
 
             @pl.when(both(first, k + 1 < n_gu))
             def _():
@@ -871,24 +886,29 @@
             def _():
                 ring_pass(L1, 1)
 
-            @pl.when(jnp.logical_not(first))
+            j = j_end + n_lead + k
+            later = jnp.logical_not(first)
+
+            @pl.when(both(later, k + n_lead < n_t))
             def _():
                 wait_out(wz, wzs.at[0])
-                j = j_end + k
                 z_step(0, wz, j)
 
-                @pl.when(k >= 1)
-                def _():
-                    rs_b(j - 1)
-
-                @pl.when(k >= 2)
-                def _():
-                    rs_c(L1, j - 2, 0, k - 2)
-
-                @pl.when(k + 1 < n_t)
-                def _():
-                    out_arrives(L1, k + 1)
-                    load_out(L1, k + 1, wz, wzs.at[0])
+            @pl.when(both(later, k + n_lead <= n_t))
+            def _():
+                rs_b(j - 1)
+
+            @pl.when(later)
+            def _():
+                rs_c(L1, j - 2, 0, k)
+
+            @pl.when(later)
+            def _():
+                z_next(k + n_lead + 1)
+
+            @pl.when(both(first, k == n_gu - 1))
+            def _():
+                z_next(0)
         loop(n_gu, gu)
 
     loop(nb, stage1)
@@ -905,9 +925,14 @@
             load_out(L1, t + 1, *wslot_of(1 - wslot))
         j = j_end + n_t + t
         z_step(1, wv.at[wslot], j)
-        rs_b(j - 1)
-        i2 = n_t + t - 2
-        rs_c(L1, j - 2, lax.div(i2, n_t), lax.rem(i2, n_t))
+
+        @pl.when(t >= 1)
+        def _():
+            rs_b(j - 1)
+
+        @pl.when(t >= 2)
+        def _():
+            rs_c(L1, j - 2, 1, t - 2)
 
     loop(n_t, z_loop1)
     j_last = 2 * j_end - 1

time: 750 us -> 749 us (level)
  no operation moved by 1% of the time
where the time goes in v3:
time: 749 us; the launch traced here: 739 us
  Pallas kernels  733 us (98%)
    pallas_call x1, Pallas kernels, device_step(): pl.pallas_call(functools.partial(kernel, cfg), out_shape=[jax.ShapeDtypeS...  733 us

profile of v3, /device:TPU:97, one launch (start us, length us, event | category | flops | bytes accessed | tf_op | source)
XLA Modules:
  0.0 738.8 jit_solution(2817799275441487469)
XLA Ops:
  0.0 1.3 broadcast_in_dim.2.kl_ref
  1.3 1.3 convert_element_type.3.gain_ref
  2.6 733.0 %shard_map.64 = (bf16[2,128,4096]{2,1,0:T(8,128)(2,1)}, bf16[2,4,1024,4864]{3,2,1,0:T(8,128)(2,1)}, bf16[2,4,512,1024]{3,2,1,0:T(8,128)(2,1)}, bf16[2,4,2048,1024]{3,2,1,0:T(8,128)(2,1)}) custom-call(bf16[2,128,4096]{2,1,0:T(8,128)(2,1)} %x_ref.1, s32[2,8,128]{2,1,0:T(8,128)} %broadcast_in_dim.2.kl_ref, f32[2,1024]{1,0:T(2,128)} %convert_element_type.3.gain_ref, ...), custom_call_target="tpu_custom_call" | custom-call | tf_op jit(solution)/shard_map/pallas_call | solution.py:989
  735.6 3.1 copy.8
